TPU v7x, 32 devices: a whole 2x2x4 slice. The times are simulated.
32 devices in a mesh: row: 2 (over y), phi: 16 (over z, x, core).
Axes of the slice: x: 2, y: 2, z: 4, core: 2. Of those that a mesh axis runs over, the one named last changes fastest.
Arguments:
- density: float32 [32, 2048, 512], P('row', 'phi'), may hold values from 0.3 to 3
- velocity: float32 [3, 32, 2048, 512], P(None, 'row', 'phi'), may hold values from -3 to 3
- magnetic: float32 [3, 32, 2048, 512], P(None, 'row', 'phi'), may hold values from -6 to 6
Outputs:
- density_next: float32 [32, 2048, 512], P('row', 'phi')
- magnetic_next: float32 [3, 32, 2048, 512], P(None, 'row', 'phi')
All inputs are finite; a program needn't handle non-finite values.
Results may differ from a plain program's by a relative error of at most 0.0003.
Values sent between devices are 32-bit elements; how exact they have to be, the bound alone decides.
A program may use at most 256 MiB of HBM per device.

v0:
```python
import math

import jax
import jax.numpy as jnp
import numpy as np
from jax import lax
from jax.experimental import pallas as pl
from jax.experimental.pallas import tpu as pltpu
from jax.sharding import PartitionSpec as P


NPOL = 128
RADIX = 16
FRONT = 16
TILE = 8
HALO = 8
REACH = 3

COURANT_RAD = 0.3
COURANT_POL = 0.25
COURANT_AZI = 0.35
SOUND_SPEED = 1.0


def rotate(value, angle):
    re, im = value
    c, s = math.cos(angle), math.sin(angle)
    if im is None:
        return (re * c, re * s)
    return (re * c - im * s, re * s + im * c)


def add(a, b, sign=1.0):
    def part(x, y):
        if y is None:
            return x
        if x is None:
            return y if sign > 0 else -y
        return x + y if sign > 0 else x - y

    return (part(a[0], b[0]), part(a[1], b[1]))


def conj(a):
    return (a[0], None if a[1] is None else -a[1])


def real_fft(xs):
    n = len(xs)
    if n == 1:
        return [(xs[0], None)]
    if n == 2:
        return [(xs[0] + xs[1], None), (xs[0] - xs[1], None)]
    even, odd = real_fft(xs[0::2]), real_fft(xs[1::2])
    half = n // 2

    def at(spec, k):
        return spec[k] if k <= half // 2 else conj(spec[half - k])

    result = []
    for k in range(half + 1):
        e, o = at(even, k % half), at(odd, k % half)
        if k == 0:
            result.append(add(e, o))
        elif k == half:
            result.append(add(e, o, -1.0))
        elif 4 * k == n:
            result.append((e[0], -o[0]))
        else:
            result.append(add(e, rotate(o, -2.0 * math.pi * k / n)))
    return result


def real_ifft(spec, n):
    if n == 2:
        a, b = spec[0][0], spec[1][0]
        return [a + b, a - b]
    half = n // 2
    even, odd = [], []
    for k in range(half // 2 + 1):
        a, b = spec[k], conj(spec[half - k])
        if k == 0:
            a, b = (spec[0][0], None), (spec[half][0], None)
            even.append(add(a, b))
            odd.append(add(a, b, -1.0))
        elif 4 * k == n:
            even.append((2.0 * spec[k][0], None))
            odd.append((-2.0 * spec[k][1], None))
        else:
            even.append(add(a, b))
            odd.append(rotate(add(a, b, -1.0), 2.0 * math.pi * k / n))
    evens, odds = real_ifft(even, half), real_ifft(odd, half)
    return [v for pair in zip(evens, odds) for v in pair]


def filter_tables(cells, theta_count):
    inner = cells // RADIX
    half_polar = NPOL // 2
    k2 = np.arange(RADIX // 2 + 1)[:, None]
    mode = k2 + RADIX * np.arange(inner)[None, :]
    angle = 2.0 * np.pi / cells * ((mode[:, :, None] * np.arange(inner)) % cells)
    cos, sin = np.cos(angle), np.sin(angle)
    forward = np.concatenate(
        [np.concatenate([cos, sin], 2), np.concatenate([-sin, cos], 2)], 1
    ).astype(np.float32)
    rows = np.arange(NPOL)
    theta = np.where(rows < half_polar, rows, theta_count - NPOL + rows)
    row_square = np.sin(np.pi * (theta + 0.5) / theta_count) ** 2
    edge = np.sin(np.pi * (half_polar + 0.5) / theta_count)
    mode_square = (edge * np.sin(np.pi * mode / cells)) ** 2
    damping = row_square / np.maximum(row_square, mode_square[:, :, None])
    return forward, (damping / cells).astype(np.float32)


def filter_kernel(group, inner, blocks, x_ref, basis_ref, damp_ref, out_ref):
    devices, _, azimuth, _ = x_ref.shape

    def slab(d):
        parts = [
            x_ref[d * blocks : (d + 1) * blocks, g].reshape(inner, NPOL) for g in range(group)
        ]
        return jnp.concatenate(parts, axis=1) if group > 1 else parts[0]

    spectrum = real_fft([slab(d) for d in range(RADIX)])
    filtered = []
    for k, (re, im) in enumerate(spectrum):
        basis = basis_ref[k]
        if im is None:
            forward = basis[:, :inner]
            stacked = re
        else:
            forward = basis
            stacked = jnp.concatenate([re, im], axis=0)
        modes = jnp.dot(
            forward, stacked, precision=lax.Precision.HIGHEST, preferred_element_type=jnp.float32
        )
        damp = damp_ref[k]
        damp = jnp.concatenate([damp, damp], axis=0)
        if group > 1:
            damp = jnp.concatenate([damp] * group, axis=1)
        back = lax.dot_general(
            forward,
            modes * damp,
            (((0,), (0,)), ((), ())),
            precision=lax.Precision.HIGHEST,
            preferred_element_type=jnp.float32,
        )
        filtered.append((back, None) if im is None else (back[:inner], back[inner:]))
    for d, value in enumerate(real_ifft(filtered, RADIX)):
        for g in range(group):
            out_ref[d * blocks : (d + 1) * blocks, g, :azimuth] = value[
                :, g * NPOL : (g + 1) * NPOL
            ].reshape(blocks, azimuth, NPOL)
    blank = jnp.zeros((HALO - 2 * REACH, NPOL), jnp.float32)
    for d in range(devices):
        for g in range(group):
            below = out_ref[(d - 1) % devices, g, azimuth - REACH : azimuth]
            above = out_ref[(d + 1) % devices, g, :REACH]
            out_ref[d, g, azimuth:] = jnp.concatenate([below, above, blank], axis=0)


def filter_lines(lines, theta_count):
    devices, pairs, azimuth, _ = lines.shape
    cells = devices * azimuth
    inner = cells // RADIX
    blocks = inner // azimuth
    group = 2 if pairs % 2 == 0 else 1
    forward, damping = filter_tables(cells, theta_count)
    spec = pl.BlockSpec((devices, group, azimuth, NPOL), lambda p: (0, p, 0, 0))
    out = pl.BlockSpec((devices, group, azimuth + HALO, NPOL), lambda p: (0, p, 0, 0))
    return pl.pallas_call(
        lambda *refs: filter_kernel(group, inner, blocks, *refs),
        grid=(pairs // group,),
        in_specs=[
            spec,
            pl.BlockSpec(forward.shape, lambda p: (0, 0, 0)),
            pl.BlockSpec(damping.shape, lambda p: (0, 0, 0)),
        ],
        out_specs=out,
        out_shape=jax.ShapeDtypeStruct((devices, pairs, azimuth + HALO, NPOL), jnp.float32),
        compiler_params=pltpu.CompilerParams(vmem_limit_bytes=56 * 1024 * 1024),
        cost_estimate=pl.CostEstimate(
            flops=32 * inner * cells * NPOL * pairs, bytes_accessed=8 * lines.size, transcendentals=0
        ),
        name="polar_filter",
    )(lines, jnp.asarray(forward), jnp.asarray(damping))


def pack_lines(density, velocity, first, layers):
    _, azimuth, width = density.shape
    half = NPOL // 2
    last = width // NPOL - 1
    step = 2 if layers % 2 == 0 else 1

    def kernel(start, d0, d1, v0, v1, out):
        lane = lax.broadcasted_iota(jnp.int32, (azimuth, NPOL), 1)
        for i in range(step):
            out[0, i] = jnp.where(lane < half, d0[i], d1[i])
            for c in range(3):
                out[1 + c, i] = jnp.where(lane < half, v0[c, i], v1[c, i])

    def dens(tile):
        return pl.BlockSpec((step, azimuth, NPOL), lambda t, s: (s[0] + t, 0, tile))

    def vel(tile):
        return pl.BlockSpec((3, step, azimuth, NPOL), lambda t, s: (0, s[0] + t, 0, tile))

    return pl.pallas_call(
        kernel,
        grid_spec=pltpu.PrefetchScalarGridSpec(
            num_scalar_prefetch=1,
            grid=(layers // step,),
            in_specs=[dens(0), dens(last), vel(0), vel(last)],
            out_specs=pl.BlockSpec((4, step, azimuth, NPOL), lambda t, s: (0, t, 0, 0)),
        ),
        out_shape=jax.ShapeDtypeStruct((4, layers, azimuth, NPOL), jnp.float32),
        name="pack_lines",
    )(jnp.reshape(first // step, (1,)), density, density, velocity, velocity)


def pack_sides(density, velocity, magnetic):
    radial, azimuth, width = density.shape
    last = azimuth // TILE - 1
    step = 4 if radial % 4 == 0 else 1

    def kernel(d0, d1, v0, v1, m0, m1, low, high):
        def rows(i, dens, vel, mag, pick, wide):
            parts = [dens[i, pick(REACH)], vel[2, i, pick(REACH)], vel[0, i, pick(1)], vel[1, i, pick(1)]]
            parts += [mag[0, i, pick(1)], mag[1, i, pick(1)], mag[2, i, pick(wide)]]
            used = sum(p.shape[0] for p in parts)
            parts.append(jnp.zeros((PACKED - used, width), jnp.float32))
            return jnp.concatenate(parts, axis=0)

        for i in range(step):
            low[i] = rows(i, d0, v0, m0, lambda n: slice(0, n), 2)
            high[i] = rows(i, d1, v1, m1, lambda n: slice(TILE - n, TILE), 1)

    def three(b):
        return pl.BlockSpec((3, step, TILE, width), lambda t: (0, t, b, 0))

    def one(b):
        return pl.BlockSpec((step, TILE, width), lambda t: (t, b, 0))

    return pl.pallas_call(
        kernel,
        grid=(radial // step,),
        in_specs=[one(0), one(last), three(0), three(last), three(0), three(last)],
        out_specs=[pl.BlockSpec((step, PACKED, width), lambda t: (t, 0, 0))] * 2,
        out_shape=[jax.ShapeDtypeStruct((radial, PACKED, width), jnp.float32)] * 2,
        name="pack_sides",
    )(density, density, velocity, velocity, magnetic, magnetic)


def interface_value(outer_left, inner_left, inner_right, outer_right):
    guess = 7.0 / 12.0 * (inner_left + inner_right) - 1.0 / 12.0 * (outer_left + outer_right)
    low = jnp.minimum(inner_left, inner_right)
    return jnp.minimum(jnp.maximum(guess, low), jnp.maximum(inner_left, inner_right))


def limited(centre, left_face, right_face):
    to_left = left_face - centre
    to_right = right_face - centre
    reach_right = 2.0 * jnp.abs(to_right)
    reach_left = 2.0 * jnp.abs(to_left)
    left = jnp.minimum(jnp.maximum(to_left, -reach_right), reach_right)
    right = jnp.minimum(jnp.maximum(to_right, -reach_left), reach_left)
    return centre + left, centre + right


def edges(q):
    left_face = interface_value(q[0], q[1], q[2], q[3])
    right_face = interface_value(q[1], q[2], q[3], q[4])
    return limited(q[2], left_face, right_face)


def hll_flux(dens_left, dens_right, speed_left, speed_right):
    slowest = jnp.minimum(jnp.minimum(speed_left, speed_right) - SOUND_SPEED, 0.0)
    fastest = jnp.maximum(jnp.maximum(speed_left, speed_right) + SOUND_SPEED, 0.0)
    upwind = fastest * dens_left * speed_left - slowest * dens_right * speed_right
    return (upwind + slowest * fastest * (dens_right - dens_left)) / (fastest - slowest)


PRIM_ROWS = ((0, 0, 3), (3, 3, 3), (1, 6, 1), (2, 7, 1))
MAG_ROWS_LOW = ((4, 8, 1), (5, 9, 1), (6, 10, 1))
MAG_ROWS_HIGH = ((4, 8, 1), (5, 9, 1), (6, 10, 2))
PACKED = 16


def stencil_kernel(middle, radial, azimuth, chunk, starts, refs, ghosts, outs, scratch):
    (s0, s1, s2, s3, s4, s5, s6, er, et, ep, carry_rho, carry_u, carry_flux) = scratch
    state = (s0, s1, s2, s3, s4, s5, s6)
    t = pl.program_id(0)
    width = s0.shape[-1]
    half = NPOL // 2
    slot = lax.rem(t, 8)
    layer = starts[0] + t - 3
    own = slice(FRONT, FRONT + azimuth)
    dens_out, mag_out = outs

    def low_lanes(rows):
        return lax.broadcasted_iota(jnp.int32, (rows, NPOL), 1) < half

    def ring(x):
        full = x.shape[1]
        mixed = jnp.where(low_lanes(x.shape[0]), x[:, full - NPOL :], x[:, :NPOL])
        return jnp.concatenate([x[:, NPOL : full - NPOL], mixed], axis=1)

    def outer(x, pol=None):
        lanes = low_lanes(x.shape[0])
        a, b = x[:, :NPOL], x[:, x.shape[1] - NPOL :]
        if pol is not None:
            a, b = jnp.where(lanes, pol, a), jnp.where(lanes, b, pol)
        return jnp.concatenate([a, b], axis=1)

    edge = azimuth + REACH

    def fill(fields, pols, low, high):
        for f, x in enumerate(fields):
            if middle:
                state[f][slot, own] = ring(x())
            elif f < 4:
                state[f][slot, own] = outer(x(), pols[f][:azimuth])
            else:
                state[f][slot, own] = outer(x())
        for f, row, n in PRIM_ROWS:
            a, b = low[row : row + n], high[row : row + n]
            if middle:
                a, b = ring(a), ring(b)
            else:
                a = outer(a, pols[f][edge - n : edge])
                b = outer(b, pols[f][edge : edge + n])
            state[f][slot, FRONT - n : FRONT] = a
            state[f][slot, FRONT + azimuth : FRONT + azimuth + n] = b
        shape = ring if middle else outer
        for f, row, n in MAG_ROWS_LOW:
            state[f][slot, FRONT - n : FRONT] = shape(low[row : row + n])
        for f, row, n in MAG_ROWS_HIGH:
            state[f][slot, FRONT + azimuth : FRONT + azimuth + n] = shape(high[row : row + n])

    mid_dens = mid_mag = None
    if middle:
        dens, vel, mag, side_low, side_high = refs
        fields = [lambda: dens[0]]
        fields += [lambda c=c: vel[c, 0] for c in range(3)]
        fields += [lambda c=c: mag[c, 0] for c in range(3)]
        choices = [(None, None)]
    else:
        d0, d1, v0, v1, m0, m1, pols, side_low, side_high, mid_dens, mid_mag = refs

        def both(a, b):
            return jnp.concatenate([a, b], axis=1)

        fields = [lambda: both(d0[0], d1[0])]
        fields += [lambda c=c: both(v0[c, 0], v1[c, 0]) for c in range(3)]
        fields += [lambda c=c: both(m0[c, 0], m1[c, 0]) for c in range(3)]
        choices = []
        for i, pol in enumerate(pols):
            inside = None
            if len(pols) > 1:
                at_layer = jnp.clip(layer, 0, radial - 1) - starts[2 + i]
                inside = (at_layer >= 0) & (at_layer < chunk)
            choices.append((pol, inside))
    mine = None if ghosts is None else (layer >= 0) & (layer < radial)
    for pol, inside in choices:
        def load(pol=pol):
            pieces = None if pol is None else [pol.at[c, 0] for c in range(4)]
            fill(fields, pieces, side_low.at[0], side_high.at[0])

        cond = mine if inside is None else inside if mine is None else mine & inside
        if cond is None:
            load()
        else:
            pl.when(cond)(load)
    if ghosts is not None:
        @pl.when(jnp.logical_not(mine))
        def _():
            planes = [lambda r=r: r[0] for r in ghosts[:7]]
            pieces = [r.at[0] for r in ghosts[9:]]
            fill(planes, pieces, ghosts[7].at[0], ghosts[8].at[0])

    shape = (TILE, width)
    lane = lax.broadcasted_iota(jnp.int32, shape, 1)
    sub = lax.broadcasted_iota(jnp.int32, shape, 0)

    def shifted(ref, index, base, off):
        here = ref[index, pl.ds(base, TILE), :]
        if off > 0:
            other = ref[index, pl.ds(base + TILE, TILE), :]
            return pltpu.roll(jnp.where(sub < off, other, here), TILE - off, 0)
        if off < 0:
            other = ref[index, pl.ds(base - TILE, TILE), :]
            return pltpu.roll(jnp.where(sub >= TILE + off, other, here), -off, 0)
        return here

    def at(ref, d, base, off=0):
        return shifted(ref, lax.rem(t - 3 + d + 8, 8), base, off)

    def up(x):
        rolled = pltpu.roll(x, width - 1, 1)
        return rolled if middle else jnp.where(lane == width - 1, x, rolled)

    def down(x):
        rolled = pltpu.roll(x, 1, 1)
        return rolled if middle else jnp.where(lane == 0, x, rolled)

    def before(x, previous):
        return jnp.where(sub == 0, pltpu.roll(previous, 1, 0), pltpu.roll(x, 1, 0))

    def azimuth_step(base, right_rho, right_u):
        left_r, next_r = edges([at(s0, 0, base, o) for o in (-1, 0, 1, 2, 3)])
        left_u, next_u = edges([at(s3, 0, base, o) for o in (-1, 0, 1, 2, 3)])
        flux = hll_flux(before(next_r, right_rho), left_r, before(next_u, right_u), left_u)
        return next_r, next_u, flux

    def theta_edges(q):
        below = down(q)
        face = interface_value(down(below), below, q, up(q))
        rolled = pltpu.roll(face, width - 1, 1)
        above = rolled if middle else jnp.where(lane == width - 1, q, rolled)
        return limited(q, face, above)

    here = lax.rem(t, 4)

    def emf_tile(j, _):
        base = pl.multiple_of(FRONT - TILE + j * TILE, TILE)
        u_r, u_t, u_p = (at(s, 1, base) for s in (s1, s2, s3))
        b_r = 0.5 * (at(s4, 1, base) + at(s4, 2, base))
        b_t = at(s5, 1, base)
        b_t = 0.5 * (b_t + up(b_t))
        b_p = 0.5 * (at(s6, 1, base) + at(s6, 1, base, 1))
        rows = pl.ds(base, TILE)
        er[here, rows, :] = u_p * b_t - u_t * b_p
        et[here, rows, :] = u_r * b_p - u_p * b_r
        ep[here, rows, :] = u_t * b_r - u_r * b_t
        return 0

    @pl.when(t >= 4)
    def _():
        lax.fori_loop(0, azimuth // TILE + 2, emf_tile, 0, unroll=2)

    def emf(ref, d, base, off=0):
        return shifted(ref, lax.rem(t - 1 + d + 4, 4), base, off)

    def radial_step(rows, base):
        left_r, right_r = edges([at(s0, d, base) for d in (-1, 0, 1, 2, 3)])
        left_u, right_v = edges([at(s1, d, base) for d in (-1, 0, 1, 2, 3)])
        flux = hll_flux(carry_rho[rows, :], left_r, carry_u[rows, :], left_u)
        total = COURANT_RAD * (flux - carry_flux[rows, :])
        carry_rho[rows, :] = right_r
        carry_u[rows, :] = right_v
        carry_flux[rows, :] = flux
        return total

    def put(ref, index, rows, value, mid):
        if middle:
            ref[index + (rows, slice(None))] = value
            return
        inner = width + NPOL
        keep = lax.broadcasted_iota(jnp.int32, (TILE, NPOL), 1)
        mixed = mid[:, inner - NPOL :]
        quarter = half // 2
        first = jnp.where(keep < half + quarter, value[:, :NPOL], mixed)
        last = jnp.where(keep >= quarter, value[:, NPOL:], mixed)
        ref[index + (rows, slice(0, NPOL))] = first
        ref[index + (rows, slice(NPOL, inner))] = mid[:, : inner - NPOL]
        ref[index + (rows, slice(inner, inner + NPOL))] = last

    def middle_of(rows, c=None):
        if middle:
            return None
        return mid_dens[0, rows, :] if c is None else mid_mag[c, 0, rows, :]

    def tile(j, carry):
        right_rho, right_u, flux_low = carry
        start = pl.multiple_of(j * TILE, TILE)
        base = pl.multiple_of(FRONT + j * TILE, TILE)
        rows = pl.ds(start, TILE)

        total = radial_step(rows, base)

        right_rho, right_u, flux = azimuth_step(base, right_rho, right_u)
        total = total + COURANT_AZI * (flux - before(flux, flux_low))
        flux_low = flux

        rho = at(s0, 0, base)
        left_r, right_r = theta_edges(rho)
        left_u, right_v = theta_edges(at(s2, 0, base))
        theta_flux = hll_flux(down(right_r), left_r, down(right_v), left_u)
        if not middle:
            theta_flux = jnp.where(lane == 0, 0.0, theta_flux)
        above = pltpu.roll(theta_flux, width - 1, 1)
        if not middle:
            above = jnp.where(lane == width - 1, 0.0, above)
        total = total + COURANT_POL * (above - theta_flux)
        put(dens_out, (0,), rows, rho - total, middle_of(rows))

        er_low, er_here, er_high = (emf(er, 0, base, o) for o in (-1, 0, 1))
        ep_low, ep_here, ep_high = (emf(ep, d, base) for d in (-1, 0, 1))
        below_k = emf(et, -1, base, -1)
        edge_a = 0.5 * (ep_low + ep_here)
        edge_r = 0.5 * (er_low + er_here)
        mixed = (0.5 * COURANT_RAD) * (ep_high - ep_low) - (0.5 * COURANT_AZI) * (er_high - er_low)
        across = emf(et, -1, base, 1) + emf(et, 0, base, 1) - below_k - emf(et, 0, base, -1)
        along = emf(et, 1, base, -1) + emf(et, 1, base) - below_k - emf(et, -1, base)
        put(mag_out, (0, 0), rows,
            at(s4, 0, base)
            - (0.5 * COURANT_POL) * (up(edge_a) - down(edge_a))
            + (0.25 * COURANT_AZI) * across, middle_of(rows, 0))
        put(mag_out, (1, 0), rows, at(s5, 0, base) + 0.5 * (down(mixed) + mixed), middle_of(rows, 1))
        put(mag_out, (2, 0), rows,
            at(s6, 0, base)
            - (0.25 * COURANT_RAD) * along
            + (0.5 * COURANT_POL) * (up(edge_r) - down(edge_r)), middle_of(rows, 2))
        return right_rho, right_u, flux_low

    @pl.when((t >= 4) & (t < 6))
    def _():
        def warm(j, _):
            start = pl.multiple_of(j * TILE, TILE)
            radial_step(pl.ds(start, TILE), pl.multiple_of(FRONT + j * TILE, TILE))
            return 0

        lax.fori_loop(0, azimuth // TILE, warm, 0, unroll=2)

    @pl.when(t >= 6)
    def _():
        zero = jnp.zeros(shape, jnp.float32)
        first = azimuth_step(FRONT - TILE, zero, zero)
        lax.fori_loop(0, azimuth // TILE, tile, first, unroll=4)


def stencil(middle, count, starts, fields, sides, ghosts=None, polar=None, mids=None, into=None):
    density, velocity, magnetic = fields
    radial, azimuth, width = density.shape
    tiles = width // NPOL

    def own(t, s):
        return jnp.clip(s[0] + t - 3, 0, radial - 1)

    def out(t, s):
        return s[1] + jnp.clip(t - 6, 0, count - 1)

    def one(w, index=0):
        return pl.BlockSpec((1, azimuth, w), lambda t, s: (own(t, s), 0, index))

    def three(w, index=0):
        return pl.BlockSpec((3, 1, azimuth, w), lambda t, s: (0, own(t, s), 0, index))

    def deep(t, s):
        g = s[0] + t - 3
        return jnp.clip(jnp.where(g < 0, g + 3, g - radial), 0, 2)

    def two(t, s):
        g = s[0] + t - 3
        return jnp.clip(jnp.where(g < 0, g + 2, g - radial), 0, 1)

    side = pl.BlockSpec((1, PACKED, width), lambda t, s: (own(t, s), 0, 0))
    chunk = 0
    if middle:
        ring = width - NPOL
        out_width = ring
        args = [density, velocity, magnetic, *sides]
        specs = [one(width), three(width), three(width), side, side]
    else:
        ring = 2 * NPOL
        out_width = width
        chunk = polar[0].shape[1]
        args = [density, density, velocity, velocity, magnetic, magnetic, *polar, *sides, *mids]
        specs = [one(NPOL), one(NPOL, tiles - 1), three(NPOL), three(NPOL, tiles - 1),
                 three(NPOL), three(NPOL, tiles - 1)]
        for i, p in enumerate(polar):
            specs.append(pl.BlockSpec(
                (4, 1, azimuth + HALO, NPOL),
                lambda t, s, i=i: (0, jnp.clip(own(t, s) - s[2 + i], 0, chunk - 1), 0, 0)))
        specs += [side, side]
        mid_width = width - NPOL
        specs += [pl.BlockSpec((1, azimuth, mid_width), lambda t, s: (out(t, s), 0, 0)),
                  pl.BlockSpec((3, 1, azimuth, mid_width), lambda t, s: (0, out(t, s), 0, 0))]
    used = len(args)
    extra = 0
    if ghosts is not None:
        planes, corner, filtered = ghosts
        where = [lambda t, s: deep(t, s), lambda t, s: 3 + deep(t, s), lambda t, s: 6, lambda t, s: 7]
        index = where + [lambda t, s: 8 + two(t, s), lambda t, s: 10, lambda t, s: 11]
        for f in index:
            args.append(planes)
            specs.append(pl.BlockSpec((1, azimuth, width), lambda t, s, f=f: (f(t, s), 0, 0)))
        for first in (0, 2):
            args.append(corner)
            specs.append(pl.BlockSpec(
                (1, PACKED, width), lambda t, s, first=first: (first + two(t, s), 0, 0)))
        if filtered is not None:
            for f in where:
                args.append(filtered)
                specs.append(pl.BlockSpec(
                    (1, azimuth + HALO, NPOL), lambda t, s, f=f: (f(t, s), 0, 0)))
        extra = len(args) - used
    aliases = {}
    if into is not None:
        for i, x in enumerate(into):
            aliases[1 + len(args)] = i
            args.append(x)
            specs.append(pl.BlockSpec(memory_space=pl.ANY))

    def kernel(starts, *refs):
        ins, outs, scratch = refs[:used], refs[len(args) : len(args) + 2], refs[len(args) + 2 :]
        spare = refs[used : used + extra] if extra else None
        if not middle:
            n = len(polar)
            ins = ins[:6] + (ins[6 : 6 + n],) + ins[6 + n :]
        stencil_kernel(middle, radial, azimuth, chunk, starts, ins, spare, outs, scratch)

    rows = FRONT + azimuth + 2 * TILE
    scratch = (
        [pltpu.VMEM((8, rows, ring), jnp.float32)] * 7
        + [pltpu.VMEM((4, rows, ring), jnp.float32)] * 3
        + [pltpu.VMEM((azimuth, ring), jnp.float32)] * 3
    )
    return pl.pallas_call(
        kernel,
        grid_spec=pltpu.PrefetchScalarGridSpec(
            num_scalar_prefetch=1,
            grid=(count + 6,),
            in_specs=specs,
            out_specs=[
                pl.BlockSpec((1, azimuth, out_width), lambda t, s: (out(t, s), 0, 0)),
                pl.BlockSpec((3, 1, azimuth, out_width), lambda t, s: (0, out(t, s), 0, 0)),
            ],
            scratch_shapes=scratch,
        ),
        out_shape=[
            jax.ShapeDtypeStruct((radial, azimuth, out_width), jnp.float32),
            jax.ShapeDtypeStruct((3, radial, azimuth, out_width), jnp.float32),
        ],
        input_output_aliases=aliases,
        compiler_params=pltpu.CompilerParams(
            dimension_semantics=("arbitrary",), vmem_limit_bytes=62 * 1024 * 1024
        ),
        cost_estimate=pl.CostEstimate(
            flops=1000 * count * azimuth * ring, bytes_accessed=48 * count * azimuth * width,
            transcendentals=0,
        ),
        name="section_mid" if middle else "section_polar",
    )(starts, *args)


def swap_rows(x):
    return lax.ppermute(x, "row", [(0, 1), (1, 0)])


def section(density, velocity, magnetic):
    radial, azimuth, width = density.shape
    devices = lax.axis_size("phi")
    pairs = 4 * radial // devices
    chunks = 2 if pairs % 2 == 0 else 1
    layers = radial // chunks
    low = lax.axis_index("row") == 0
    fields = (density, velocity, magnetic)

    def pick(a, b):
        return jnp.where(low, jnp.int32(a), jnp.int32(b))

    def transpose(x, rows):
        x = x.reshape(devices, pairs // chunks, rows, NPOL)
        return lax.all_to_all(x, "phi", split_axis=0, concat_axis=0, tiled=True)

    base = [pick(layers * (chunks - 1 - c), layers * c) for c in range(chunks)]
    packed = [pack_lines(density, velocity, base[c], layers) for c in range(chunks)]
    first_rows, last_rows = pack_sides(density, velocity, magnetic)

    far, near, pair = pick(radial - 3, 0), pick(radial - 1, 0), pick(radial - 2, 0)

    def plane(x, c, n, start, size):
        return lax.dynamic_slice(x, (c, start, 0, 0), (n, size, azimuth, width)).reshape(
            n * size, azimuth, width)

    planes = jnp.concatenate(
        [lax.dynamic_slice_in_dim(density, far, 3, 0), plane(velocity, 0, 1, far, 3),
         plane(velocity, 1, 2, near, 1), plane(magnetic, 0, 1, pair, 2),
         plane(magnetic, 1, 2, near, 1)], axis=0)
    around = [(i, (i + 1) % devices) for i in range(devices)]
    back = [(j, i) for i, j in around]

    lines = [transpose(packed[0], azimuth)]
    sides = (lax.ppermute(last_rows, "phi", around), lax.ppermute(first_rows, "phi", back))
    if chunks > 1:
        packed[1], sides, planes = lax.optimization_barrier((packed[1], sides, planes))
        lines.append(transpose(packed[1], azimuth))
    planes = swap_rows(planes)
    corner = swap_rows(
        jnp.concatenate([lax.dynamic_slice_in_dim(x, pair, 2, 0) for x in sides], axis=0))

    def starts(s):
        return jnp.stack([s, s] + base)

    deep = radial - REACH
    early = (deep + 1) // 2
    mids = stencil(True, early, starts(pick(0, REACH)), fields, sides)
    smooth = [filter_lines(x, width) for x in lines]
    smooth[0], mids = lax.optimization_barrier((smooth[0], tuple(mids)))
    polar = [transpose(smooth[0], azimuth + HALO)]
    mids = stencil(True, deep - early, starts(pick(early, early + REACH)), fields, sides, into=mids)
    if chunks > 1:
        smooth[1], mids = lax.optimization_barrier((smooth[1], tuple(mids)))
        polar.append(transpose(smooth[1], azimuth + HALO))
    polar = [p.reshape(4, layers, azimuth + HALO, NPOL) for p in polar]

    first = polar[0]
    far, near = pick(layers - 3, 0), pick(layers - 1, 0)
    sent = lax.dynamic_slice_in_dim(first[:2], far, 3, 1).reshape(6, azimuth + HALO, NPOL)
    close = lax.dynamic_slice_in_dim(first[2:], near, 1, 1).reshape(2, azimuth + HALO, NPOL)
    filtered = swap_rows(jnp.concatenate([sent, close], axis=0))
    mids = stencil(True, REACH, starts(pick(deep, 0)), fields, sides,
                   ghosts=(planes, corner, None), into=mids)

    edge = radial // 2 - REACH
    out = stencil(False, edge, starts(pick(radial - edge, 0)), fields, sides,
                  ghosts=(planes, corner, filtered), polar=polar[:1], mids=mids)
    if chunks > 1:
        polar[1], out = lax.optimization_barrier((polar[1], tuple(out)))
    out = stencil(False, radial - edge, starts(pick(0, edge)), fields, sides, polar=polar,
                  mids=mids, into=out)
    return tuple(out)


def solution(mesh):
    placed = (P("row", "phi", None), P(None, "row", "phi", None), P(None, "row", "phi", None))
    return jax.shard_map(
        section,
        mesh=mesh,
        in_specs=placed,
        out_specs=(P("row", "phi", None), P(None, "row", "phi", None)),
        check_vma=False,
    )
```

profile of v0, /device:TPU:0, one launch (start us, length us, event | category | flops | bytes accessed | tf_op | source)
XLA Modules:
  0.0 360.6 jit_solution(9971146305505301018)
XLA Ops:
  0.6 4.3 %pack_lines.2 = f32[4,8,128,128]{3,2,1,0:T(8,128)} custom-call(s32[1]{0:T(128)} %bitcast.3.start, f32[16,128,512]{2,1,0:T(8,128)} %refs_1_.11, f32[16,128,512]{2,1,0:T(8,128)} %refs_1_.11, f32[3,16,128,512]{3,2,1,0:T(8,128)} %refs_3_.3, f32[3,16,128,512]{3,2,1,0:T(8,128)} %refs_3_.3), custom_call_target="tpu_custom_call" | custom-call | tf_op jit(solution)/shard_map/pack_lines/pallas_call | solution.py:208
  5.0 7.4 %all-to-all-start = ((f32[16,2,128,128]{3,2,1,0:T(8,128)}), f32[16,2,128,128]{3,2,1,0:T(8,128)}, u32[]{:S(2)}, u32[]{:S(2)}) async-start(f32[16,2,128,128]{3,2,1,0:T(8,128)} %bitcast.28), calls=%async_computation | async-start | bytes 4194304 | tf_op jit(solution)/shard_map/all_to_all | solution.py:665
  12.4 4.0 %pack_sides.1 = (f32[16,16,512]{2,1,0:T(8,128)}, f32[16,16,512]{2,1,0:T(8,128)}) custom-call(f32[16,128,512]{2,1,0:T(8,128)} %refs_1_.11, f32[16,128,512]{2,1,0:T(8,128)} %refs_1_.11, f32[3,16,128,512]{3,2,1,0:T(8,128)} %refs_3_.3, f32[3,16,128,512]{3,2,1,0:T(8,128)} %refs_3_.3, f32[3,16,128,512]{3,2,1,0:T(8,128)} %refs_5_.3, f32[3,16,128,512]{3,2,1,0:T(8,128)} %refs_5_.3), custom_call_target="tpu_custom_call" | custom-call | tf_op jit(solution)/shard_map/pack_sides/pallas_call | solution.py:244
  16.4 0.3 collective-permute-start
  16.8 4.1 %collective-permute-start.1 = (f32[16,16,512]{2,1,0:T(8,128)}, f32[16,16,512]{2,1,0:T(8,128)S(1)}, u32[]{:S(2)}, u32[]{:S(2)}) collective-permute-start(f32[16,16,512]{2,1,0:T(8,128)} %get-tuple-element.26), channel_id=1, source_target_pairs={{1,0},{2,1},{3,2},{4,3},{5,4},{6,5},{7,6},{8,7},{9,8},{10,9},{11,1... | collective-permute-start | bytes 1572872 | tf_op jit(solution)/shard_map/ppermute | solution.py:685
  20.9 2.1 dynamic-slice_dynamic-update-slice_fusion
  22.9 4.3 %pack_lines.3 = f32[4,8,128,128]{3,2,1,0:T(8,128)} custom-call(s32[1]{0:T(128)} %bitcast.6.start, f32[16,128,512]{2,1,0:T(8,128)} %refs_1_.11, f32[16,128,512]{2,1,0:T(8,128)} %refs_1_.11, f32[3,16,128,512]{3,2,1,0:T(8,128)} %refs_3_.3, f32[3,16,128,512]{3,2,1,0:T(8,128)} %refs_3_.3), custom_call_target="tpu_custom_call" | custom-call | tf_op jit(solution)/shard_map/pack_lines/pallas_call | solution.py:208
  27.3 2.1 bitcast_dynamic-update-slice_fusion
  29.3 1.9 bitcast_dynamic-update-slice_fusion.3
  31.2 1.9 bitcast_dynamic-update-slice_fusion.2
  33.1 1.9 bitcast_dynamic-update-slice_fusion.1
  34.9 22.9 %collective-permute-done.refs_3_.refs_7_.refs_8_ = f32[16,16,512]{2,1,0:T(8,128)S(1)} collective-permute-done((f32[16,16,512]{2,1,0:T(8,128)}, f32[16,16,512]{2,1,0:T(8,128)S(1)}, u32[]{:S(2)}, u32[]{:S(2)}) %collective-permute-start) | collective-permute-done | bytes 524320 | tf_op jit(solution)/shard_map/ppermute | solution.py:685
  57.9 0.0 copy-start
  57.9 0.0 collective-permute-done.1.refs_4_.refs_8_.refs_9_
  57.9 0.0 copy-start.1
  57.9 1.2 all-to-all-done.refs_0_
  59.0 11.4 %all-to-all-start.2 = ((f32[16,2,128,128]{3,2,1,0:T(8,128)}), f32[16,2,128,128]{3,2,1,0:T(8,128)}, u32[]{:S(2)}, u32[]{:S(2)}) async-start(f32[16,2,128,128]{3,2,1,0:T(8,128)} %bitcast.29), calls=%async_computation.2 | async-start | bytes 4194304 | tf_op jit(solution)/shard_map/all_to_all | solution.py:665
  70.4 0.6 add_add_fusion.1
  71.1 0.0 copy-done
  71.1 0.0 copy-done.1
  71.1 35.2 %section_mid.3 = (f32[16,128,384]{2,1,0:T(8,128)}, f32[3,16,128,384]{3,2,1,0:T(8,128)}) custom-call(s32[4]{0:T(128)} %get-tuple-element.50.starts, f32[16,128,512]{2,1,0:T(8,128)} %refs_1_.11, f32[3,16,128,512]{3,2,1,0:T(8,128)} %refs_3_.3, f32[3,16,128,512]{3,2,1,0:T(8,128)} %refs_5_.3, f32[16,16,512]{2,1,0:T(8,128)} %copy-done, f32[16,16,512]{2,1,0:T(8,128)} %copy-done.1), custom_call_target="tpu_custom_call" | custom-call | flops 344064000 | bytes 22020096 | tf_op jit(solution)/shard_map/section_mid/pallas_call | solution.py:619
  106.2 9.1 %polar_filter.2 = f32[16,2,136,128]{3,2,1,0:T(8,128)} custom-call(f32[16,2,128,128]{3,2,1,0:T(8,128)} %all-to-all-done.refs_0_, f32[9,256,256]{2,1,0:T(8,128)} %constant.61.clone.refs_1_, f32[9,128,128]{2,1,0:T(8,128)} %constant.62.clone.refs_2_), custom_call_target="tpu_custom_call" | custom-call | flops 2147483648 | bytes 4194304 | tf_op jit(solution)/shard_map/polar_filter/pallas_call | solution.py:171
  115.3 0.0 all-to-all-done.2.refs_0_
  115.3 7.4 %all-to-all-start.1 = ((f32[16,2,136,128]{3,2,1,0:T(8,128)}), f32[16,2,136,128]{3,2,1,0:T(8,128)}, u32[]{:S(2)}, u32[]{:S(2)}) async-start(f32[16,2,136,128]{3,2,1,0:T(8,128)} %polar_filter.2), calls=%async_computation.1 | async-start | bytes 4456448 | tf_op jit(solution)/shard_map/all_to_all | solution.py:665
  122.7 32.7 %section_mid.4 = (f32[16,128,384]{2,1,0:T(8,128)}, f32[3,16,128,384]{3,2,1,0:T(8,128)}) custom-call(s32[4]{0:T(128)} %get-tuple-element.51.starts, f32[16,128,512]{2,1,0:T(8,128)} %refs_1_.11, f32[3,16,128,512]{3,2,1,0:T(8,128)} %refs_3_.3, f32[3,16,128,512]{3,2,1,0:T(8,128)} %refs_5_.3, ...), custom_call_target="tpu_custom_call", output_to_operand_aliasing={{0}: (6, {}), {1}: (7, {})} | custom-call | flops 294912000 | bytes 18874368 | tf_op jit(solution)/shard_map/section_mid/pallas_call | solution.py:619
  155.4 9.1 %polar_filter.3 = f32[16,2,136,128]{3,2,1,0:T(8,128)} custom-call(f32[16,2,128,128]{3,2,1,0:T(8,128)} %all-to-all-done.2.refs_0_, f32[9,256,256]{2,1,0:T(8,128)} %constant.61.clone.refs_1_, f32[9,128,128]{2,1,0:T(8,128)} %constant.62.clone.refs_2_), custom_call_target="tpu_custom_call" | custom-call | flops 2147483648 | bytes 4194304 | tf_op jit(solution)/shard_map/polar_filter/pallas_call | solution.py:171
  164.5 1.5 all-to-all-done.1
  166.0 11.8 %all-to-all-start.3 = ((f32[16,2,136,128]{3,2,1,0:T(8,128)}), f32[16,2,136,128]{3,2,1,0:T(8,128)}, u32[]{:S(2)}, u32[]{:S(2)}) async-start(f32[16,2,136,128]{3,2,1,0:T(8,128)} %polar_filter.3), calls=%async_computation.3 | async-start | bytes 4456448 | tf_op jit(solution)/shard_map/all_to_all | solution.py:665
  177.8 1.6 collective-permute-start.2
  179.4 1.7 fusion
  181.3 0.6 collective-permute-start.4
  181.8 0.6 add_add_fusion.starts
  182.4 0.9 constant_dynamic-slice_fusion.1
  183.3 1.6 collective-permute-start.3
  184.9 0.6 add_add_fusion.3.starts
  185.5 0.6 add_add_fusion.4.starts
  186.1 77.0 %collective-permute-done.3.refs_12_.refs_13_.refs_18_.refs_19_ = f32[4,16,512]{2,1,0:T(8,128)S(1)} collective-permute-done((f32[4,16,512]{2,1,0:T(8,128)S(1)}, f32[4,16,512]{2,1,0:T(8,128)S(1)}, u32[]{:S(2)}, u32[]{:S(2)}) %collective-permute-start.3) | collective-permute-done | bytes 131104 | tf_op jit(solution)/shard_map/ppermute | solution.py:648
  263.1 0.0 copy-start.3
  263.1 0.0 collective-permute-done.2.refs_5_.refs_6_.refs_7_.refs_8_.refs_9_.refs_10_.refs_11_.refs_12_.refs_13_.refs_14_.refs_15_.refs_16_.refs_17_
  263.2 0.6 copy-done.3
  263.8 22.7 %section_mid.5 = (f32[16,128,384]{2,1,0:T(8,128)}, f32[3,16,128,384]{3,2,1,0:T(8,128)}) custom-call(s32[4]{0:T(128)} %add_add_fusion.4.starts, f32[16,128,512]{2,1,0:T(8,128)} %refs_1_.11, f32[3,16,128,512]{3,2,1,0:T(8,128)} %refs_3_.3, f32[3,16,128,512]{3,2,1,0:T(8,128)} %refs_5_.3, ...), custom_call_target="tpu_custom_call", output_to_operand_aliasing={{0}: (15, {}), {1}: (16, {})} | custom-call | flops 147456000 | bytes 9437184 | tf_op jit(solution)/shard_map/section_mid/pallas_call | solution.py:619
  286.5 0.0 collective-permute-done.4.refs_20_.refs_21_.refs_22_.refs_23_
  286.5 0.0 copy-start.2
  286.5 0.8 copy-done.2
  287.3 27.7 %section_polar.2 = (f32[16,128,512]{2,1,0:T(8,128)}, f32[3,16,128,512]{3,2,1,0:T(8,128)}) custom-call(s32[4]{0:T(128)} %add_add_fusion.3.starts, f32[16,128,512]{2,1,0:T(8,128)} %refs_1_.11, f32[16,128,512]{2,1,0:T(8,128)} %refs_1_.11, f32[3,16,128,512]{3,2,1,0:T(8,128)} %refs_3_.3, f32[3,16,128,512]{3,2,1,0:T(8,128)} %refs_3_.3, ...), custom_call_target="tpu_custom_call" | custom-call | flops 163840000 | bytes 15728640 | tf_op jit(solution)/shard_map/section_polar/pallas_call | solution.py:619
  315.1 0.0 all-to-all-done.3
  315.1 45.3 %section_polar.3 = (f32[16,128,512]{2,1,0:T(8,128)}, f32[3,16,128,512]{3,2,1,0:T(8,128)}) custom-call(s32[4]{0:T(128)} %add_add_fusion.starts, f32[16,128,512]{2,1,0:T(8,128)} %refs_1_.11, f32[16,128,512]{2,1,0:T(8,128)} %refs_1_.11, f32[3,16,128,512]{3,2,1,0:T(8,128)} %refs_3_.3, ...), custom_call_target="tpu_custom_call", output_to_operand_aliasing={{0}: (13, {}), {1}: (14, {})} | custom-call | flops 360448000 | bytes 34603008 | tf_op jit(solution)/shard_map/section_polar/pallas_call | solution.py:619
  (4 shorter events, 0.1 us)
Async XLA Ops:
  5.0 54.1 %all-to-all-start = ((f32[16,2,128,128]{3,2,1,0:T(8,128)}), f32[16,2,128,128]{3,2,1,0:T(8,128)}, u32[]{:S(2)}, u32[]{:S(2)}) async-start(f32[16,2,128,128]{3,2,1,0:T(8,128)} %bitcast.28), calls=%async_computation | async-start | bytes 4194304 | tf_op jit(solution)/shard_map/all_to_all | solution.py:665
  16.4 41.4 %collective-permute-start = (f32[16,16,512]{2,1,0:T(8,128)}, f32[16,16,512]{2,1,0:T(8,128)S(1)}, u32[]{:S(2)}, u32[]{:S(2)}) collective-permute-start(f32[16,16,512]{2,1,0:T(8,128)} %get-tuple-element.25), channel_id=1, source_target_pairs={{0,1},{1,2},{2,3},{3,4},{4,5},{5,6},{6,7},{7,8},{8,9},{9,10},{10,1... | collective-permute-start | bytes 1572872 | tf_op jit(solution)/shard_map/ppermute | solution.py:685
  16.8 41.1 %collective-permute-start.1 = (f32[16,16,512]{2,1,0:T(8,128)}, f32[16,16,512]{2,1,0:T(8,128)S(1)}, u32[]{:S(2)}, u32[]{:S(2)}) collective-permute-start(f32[16,16,512]{2,1,0:T(8,128)} %get-tuple-element.26), channel_id=1, source_target_pairs={{1,0},{2,1},{3,2},{4,3},{5,4},{6,5},{7,6},{8,7},{9,8},{10,9},{11,1... | collective-permute-start | bytes 1572872 | tf_op jit(solution)/shard_map/ppermute | solution.py:685
  57.9 13.2 %copy-start = (f32[16,16,512]{2,1,0:T(8,128)}, f32[16,16,512]{2,1,0:T(8,128)S(1)}, u32[]{:S(2)}) copy-start(f32[16,16,512]{2,1,0:T(8,128)S(1)} %collective-permute-done.refs_3_.refs_7_.refs_8_) | copy-start | bytes 1572868
  57.9 13.2 %copy-start.1 = (f32[16,16,512]{2,1,0:T(8,128)}, f32[16,16,512]{2,1,0:T(8,128)S(1)}, u32[]{:S(2)}) copy-start(f32[16,16,512]{2,1,0:T(8,128)S(1)} %collective-permute-done.1.refs_4_.refs_8_.refs_9_) | copy-start | bytes 1572868
  59.0 56.2 %all-to-all-start.2 = ((f32[16,2,128,128]{3,2,1,0:T(8,128)}), f32[16,2,128,128]{3,2,1,0:T(8,128)}, u32[]{:S(2)}, u32[]{:S(2)}) async-start(f32[16,2,128,128]{3,2,1,0:T(8,128)} %bitcast.29), calls=%async_computation.2 | async-start | bytes 4194304 | tf_op jit(solution)/shard_map/all_to_all | solution.py:665
  115.3 50.7 %all-to-all-start.1 = ((f32[16,2,136,128]{3,2,1,0:T(8,128)}), f32[16,2,136,128]{3,2,1,0:T(8,128)}, u32[]{:S(2)}, u32[]{:S(2)}) async-start(f32[16,2,136,128]{3,2,1,0:T(8,128)} %polar_filter.2), calls=%async_computation.1 | async-start | bytes 4456448 | tf_op jit(solution)/shard_map/all_to_all | solution.py:665
  166.0 149.1 %all-to-all-start.3 = ((f32[16,2,136,128]{3,2,1,0:T(8,128)}), f32[16,2,136,128]{3,2,1,0:T(8,128)}, u32[]{:S(2)}, u32[]{:S(2)}) async-start(f32[16,2,136,128]{3,2,1,0:T(8,128)} %polar_filter.3), calls=%async_computation.3 | async-start | bytes 4456448 | tf_op jit(solution)/shard_map/all_to_all | solution.py:665
  177.8 85.3 %collective-permute-start.2 = (f32[12,128,512]{2,1,0:T(8,128)}, f32[12,128,512]{2,1,0:T(8,128)}, u32[]{:S(2)}, u32[]{:S(2)}) collective-permute-start(f32[12,128,512]{2,1,0:T(8,128)} %bitcast_dynamic-update-slice_fusion.1), channel_id=1, source_target_pairs={{0,16},{16,0},{1,17},{17,1},{2,18},{18,2},{3,19},{19,3},{4,20},{20... | collective-permute-start | bytes 9437192 | tf_op jit(solution)/shard_map/ppermute | solution.py:648
  181.3 105.2 %collective-permute-start.4 = (f32[8,136,128]{2,1,0:T(8,128)S(1)}, f32[8,136,128]{2,1,0:T(8,128)S(1)}, u32[]{:S(2)}, u32[]{:S(2)}) collective-permute-start(f32[8,136,128]{2,1,0:T(8,128)S(1)} %pad_maximum_fusion), channel_id=1, source_target_pairs={{0,16},{16,0},{1,17},{17,1},{2,18},{18,2},{3,19},{19,3},{4,20},{20... | collective-permute-start | bytes 1671176 | tf_op jit(solution)/shard_map/ppermute | solution.py:648
  183.3 79.8 %collective-permute-start.3 = (f32[4,16,512]{2,1,0:T(8,128)S(1)}, f32[4,16,512]{2,1,0:T(8,128)S(1)}, u32[]{:S(2)}, u32[]{:S(2)}) collective-permute-start(f32[4,16,512]{2,1,0:T(8,128)S(1)} %pad_maximum_fusion.1), channel_id=1, source_target_pairs={{0,16},{16,0},{1,17},{17,1},{2,18},{18,2},{3,19},{19,3},{4,20},{20... | collective-permute-start | bytes 393224 | tf_op jit(solution)/shard_map/ppermute | solution.py:648
  263.1 0.6 copy-start.3
  286.5 0.8 copy-start.2
where the time goes:
time: 362 us; the launch traced here: 361 us
  Pallas kernels  194 us (54%)
  waiting for transfers between devices  103 us (28%)
  starting transfers between devices  46.2 us (13%)
  local copies, waits for them, and re-layouts  13.9 us (4%)
    pallas_call x5, Pallas kernels, stencil(): pl.pallas_call(kernel, grid_spec=pltpu.PrefetchScalarGridSpec(num_scalar_...  164 us
    ppermute x3, waiting for transfers between devices, swap_rows(): return lax.ppermute(x, 'row', [(0, 1), (1, 0)])  77.1 us
    all_to_all x4, starting transfers between devices, transpose(): return lax.all_to_all(x, 'phi', split_axis=0, concat_axis=0, tiled=True)  38 us
    ppermute x1, waiting for transfers between devices, section(): lax.ppermute(last_rows, 'phi', around)  22.9 us
    pallas_call x2, Pallas kernels, filter_lines(): pl.pallas_call(lambda *refs: filter_kernel(group, inner, blocks, *refs),...  18.1 us
    unnamed x12, local copies, waits for them, and re-layouts  9.33 us
    pallas_call x2, Pallas kernels, pack_lines(): pl.pallas_call(kernel, grid_spec=pltpu.PrefetchScalarGridSpec(num_scalar_...  8.63 us
  transfers between devices with their start and end apart: 9, of which 4 were waited for; matrix products, arithmetic and copies ran while one was open for 4% of the time, Pallas kernels for 40%

commit v1 on v0

--- a/solution.py
+++ b/solution.py
@@ -164,7 +164,7 @@
     cells = devices * azimuth
     inner = cells // RADIX
     blocks = inner // azimuth
-    group = 2 if pairs % 2 == 0 else 1
+    group = next(g for g in (3, 2, 1) if pairs % g == 0)
     forward, damping = filter_tables(cells, theta_count)
     spec = pl.BlockSpec((devices, group, azimuth, NPOL), lambda p: (0, p, 0, 0))
     out = pl.BlockSpec((devices, group, azimuth + HALO, NPOL), lambda p: (0, p, 0, 0))
@@ -190,7 +190,7 @@
     _, azimuth, width = density.shape
     half = NPOL // 2
     last = width // NPOL - 1
-    step = 2 if layers % 2 == 0 else 1
+    step = math.gcd(4, math.gcd(layers, density.shape[0]))
 
     def kernel(start, d0, d1, v0, v1, out):
         lane = lax.broadcasted_iota(jnp.int32, (azimuth, NPOL), 1)
@@ -267,17 +267,12 @@
     return centre + left, centre + right
 
 
-def edges(q):
-    left_face = interface_value(q[0], q[1], q[2], q[3])
-    right_face = interface_value(q[1], q[2], q[3], q[4])
-    return limited(q[2], left_face, right_face)
-
-
 def hll_flux(dens_left, dens_right, speed_left, speed_right):
     slowest = jnp.minimum(jnp.minimum(speed_left, speed_right) - SOUND_SPEED, 0.0)
     fastest = jnp.maximum(jnp.maximum(speed_left, speed_right) + SOUND_SPEED, 0.0)
-    upwind = fastest * dens_left * speed_left - slowest * dens_right * speed_right
-    return (upwind + slowest * fastest * (dens_right - dens_left)) / (fastest - slowest)
+    from_left = fastest * dens_left * (speed_left - slowest)
+    from_right = slowest * dens_right * (speed_right - fastest)
+    return (from_left - from_right) / (fastest - slowest)
 
 
 PRIM_ROWS = ((0, 0, 3), (3, 3, 3), (1, 6, 1), (2, 7, 1))
@@ -286,8 +281,9 @@
 PACKED = 16
 
 
-def stencil_kernel(middle, radial, azimuth, chunk, starts, refs, ghosts, outs, scratch):
-    (s0, s1, s2, s3, s4, s5, s6, er, et, ep, carry_rho, carry_u, carry_flux) = scratch
+def stencil_kernel(middle, radial, azimuth, chunks, starts, refs, ghosts, outs, scratch):
+    (s0, s1, s2, s3, s4, s5, s6, er, et, ep) = scratch[:10]
+    carry_rho, carry_u, carry_flux, face_of_rho, face_of_u = scratch[10:]
     state = (s0, s1, s2, s3, s4, s5, s6)
     t = pl.program_id(0)
     width = s0.shape[-1]
@@ -358,7 +354,7 @@
             inside = None
             if len(pols) > 1:
                 at_layer = jnp.clip(layer, 0, radial - 1) - starts[2 + i]
-                inside = (at_layer >= 0) & (at_layer < chunk)
+                inside = (at_layer >= 0) & (at_layer < chunks[i])
             choices.append((pol, inside))
     mine = None if ghosts is None else (layer >= 0) & (layer < radial)
     for pol, inside in choices:
@@ -406,11 +402,17 @@
     def before(x, previous):
         return jnp.where(sub == 0, pltpu.roll(previous, 1, 0), pltpu.roll(x, 1, 0))
 
-    def azimuth_step(base, right_rho, right_u):
-        left_r, next_r = edges([at(s0, 0, base, o) for o in (-1, 0, 1, 2, 3)])
-        left_u, next_u = edges([at(s3, 0, base, o) for o in (-1, 0, 1, 2, 3)])
-        flux = hll_flux(before(next_r, right_rho), left_r, before(next_u, right_u), left_u)
-        return next_r, next_u, flux
+    def azimuth_step(base, carry):
+        rights, lefts, kept = [], [], []
+        for field, past_face, past_right in ((s0, carry[0], carry[2]), (s3, carry[1], carry[3])):
+            q = [at(field, 0, base, o) for o in (-1, 0, 1, 2)]
+            face = interface_value(*q)
+            left, right = limited(q[1], before(face, past_face), face)
+            rights.append(before(right, past_right))
+            lefts.append(left)
+            kept.append((face, right))
+        flux = hll_flux(rights[0], lefts[0], rights[1], lefts[1])
+        return (kept[0][0], kept[1][0], kept[0][1], kept[1][1]), flux
 
     def theta_edges(q):
         below = down(q)
@@ -424,10 +426,10 @@
     def emf_tile(j, _):
         base = pl.multiple_of(FRONT - TILE + j * TILE, TILE)
         u_r, u_t, u_p = (at(s, 1, base) for s in (s1, s2, s3))
-        b_r = 0.5 * (at(s4, 1, base) + at(s4, 2, base))
+        b_r = at(s4, 1, base) + at(s4, 2, base)
         b_t = at(s5, 1, base)
-        b_t = 0.5 * (b_t + up(b_t))
-        b_p = 0.5 * (at(s6, 1, base) + at(s6, 1, base, 1))
+        b_t = b_t + up(b_t)
+        b_p = at(s6, 1, base) + at(s6, 1, base, 1)
         rows = pl.ds(base, TILE)
         er[here, rows, :] = u_p * b_t - u_t * b_p
         et[here, rows, :] = u_r * b_p - u_p * b_r
@@ -436,16 +438,22 @@
 
     @pl.when(t >= 4)
     def _():
-        lax.fori_loop(0, azimuth // TILE + 2, emf_tile, 0, unroll=2)
+        lax.fori_loop(0, azimuth // TILE + 2, emf_tile, 0, unroll=math.gcd(azimuth // TILE + 2, 6))
 
     def emf(ref, d, base, off=0):
         return shifted(ref, lax.rem(t - 1 + d + 4, 4), base, off)
 
+    def radial_face(field, base):
+        return interface_value(*(at(field, d, base) for d in (0, 1, 2, 3)))
+
     def radial_step(rows, base):
-        left_r, right_r = edges([at(s0, d, base) for d in (-1, 0, 1, 2, 3)])
-        left_u, right_v = edges([at(s1, d, base) for d in (-1, 0, 1, 2, 3)])
+        face_rho, face_u = radial_face(s0, base), radial_face(s1, base)
+        left_r, right_r = limited(at(s0, 1, base), face_of_rho[rows, :], face_rho)
+        left_u, right_v = limited(at(s1, 1, base), face_of_u[rows, :], face_u)
         flux = hll_flux(carry_rho[rows, :], left_r, carry_u[rows, :], left_u)
         total = COURANT_RAD * (flux - carry_flux[rows, :])
+        face_of_rho[rows, :] = face_rho
+        face_of_u[rows, :] = face_u
         carry_rho[rows, :] = right_r
         carry_u[rows, :] = right_v
         carry_flux[rows, :] = flux
@@ -471,15 +479,16 @@
         return mid_dens[0, rows, :] if c is None else mid_mag[c, 0, rows, :]
 
     def tile(j, carry):
-        right_rho, right_u, flux_low = carry
+        kept, flux_low = carry
         start = pl.multiple_of(j * TILE, TILE)
         base = pl.multiple_of(FRONT + j * TILE, TILE)
         rows = pl.ds(start, TILE)
 
         total = radial_step(rows, base)
 
-        right_rho, right_u, flux = azimuth_step(base, right_rho, right_u)
-        total = total + COURANT_AZI * (flux - before(flux, flux_low))
+        kept, flux = azimuth_step(base + TILE, kept)
+        flux_high = pltpu.roll(jnp.where(sub < 1, flux, flux_low), TILE - 1, 0)
+        total = total + COURANT_AZI * (flux_high - flux_low)
         flux_low = flux
 
         rho = at(s0, 0, base)
@@ -497,21 +506,32 @@
         er_low, er_here, er_high = (emf(er, 0, base, o) for o in (-1, 0, 1))
         ep_low, ep_here, ep_high = (emf(ep, d, base) for d in (-1, 0, 1))
         below_k = emf(et, -1, base, -1)
-        edge_a = 0.5 * (ep_low + ep_here)
-        edge_r = 0.5 * (er_low + er_here)
-        mixed = (0.5 * COURANT_RAD) * (ep_high - ep_low) - (0.5 * COURANT_AZI) * (er_high - er_low)
+        edge_a = ep_low + ep_here
+        edge_r = er_low + er_here
+        mixed = (0.125 * COURANT_RAD) * (ep_high - ep_low) - (0.125 * COURANT_AZI) * (er_high - er_low)
         across = emf(et, -1, base, 1) + emf(et, 0, base, 1) - below_k - emf(et, 0, base, -1)
         along = emf(et, 1, base, -1) + emf(et, 1, base) - below_k - emf(et, -1, base)
         put(mag_out, (0, 0), rows,
             at(s4, 0, base)
-            - (0.5 * COURANT_POL) * (up(edge_a) - down(edge_a))
-            + (0.25 * COURANT_AZI) * across, middle_of(rows, 0))
-        put(mag_out, (1, 0), rows, at(s5, 0, base) + 0.5 * (down(mixed) + mixed), middle_of(rows, 1))
+            - (0.125 * COURANT_POL) * (up(edge_a) - down(edge_a))
+            + (0.125 * COURANT_AZI) * across, middle_of(rows, 0))
+        put(mag_out, (1, 0), rows, at(s5, 0, base) + (down(mixed) + mixed), middle_of(rows, 1))
         put(mag_out, (2, 0), rows,
             at(s6, 0, base)
-            - (0.25 * COURANT_RAD) * along
-            + (0.5 * COURANT_POL) * (up(edge_r) - down(edge_r)), middle_of(rows, 2))
-        return right_rho, right_u, flux_low
+            - (0.125 * COURANT_RAD) * along
+            + (0.125 * COURANT_POL) * (up(edge_r) - down(edge_r)), middle_of(rows, 2))
+        return kept, flux_low
+
+    @pl.when(t == 3)
+    def _():
+        def warm_face(j, _):
+            rows = pl.ds(pl.multiple_of(j * TILE, TILE), TILE)
+            base = pl.multiple_of(FRONT + j * TILE, TILE)
+            face_of_rho[rows, :] = radial_face(s0, base)
+            face_of_u[rows, :] = radial_face(s1, base)
+            return 0
+
+        lax.fori_loop(0, azimuth // TILE, warm_face, 0, unroll=2)
 
     @pl.when((t >= 4) & (t < 6))
     def _():
@@ -525,8 +545,10 @@
     @pl.when(t >= 6)
     def _():
         zero = jnp.zeros(shape, jnp.float32)
-        first = azimuth_step(FRONT - TILE, zero, zero)
-        lax.fori_loop(0, azimuth // TILE, tile, first, unroll=4)
+        kept, _ = azimuth_step(FRONT - TILE, (zero, zero, zero, zero))
+        first = azimuth_step(FRONT, kept)
+        unroll = math.gcd(azimuth // TILE, 4 if middle else 8)
+        lax.fori_loop(0, azimuth // TILE, tile, first, unroll=unroll)
 
 
 def stencil(middle, count, starts, fields, sides, ghosts=None, polar=None, mids=None, into=None):
@@ -555,7 +577,7 @@
         return jnp.clip(jnp.where(g < 0, g + 2, g - radial), 0, 1)
 
     side = pl.BlockSpec((1, PACKED, width), lambda t, s: (own(t, s), 0, 0))
-    chunk = 0
+    chunks = []
     if middle:
         ring = width - NPOL
         out_width = ring
@@ -564,14 +586,14 @@
     else:
         ring = 2 * NPOL
         out_width = width
-        chunk = polar[0].shape[1]
+        chunks = [p.shape[1] for p in polar]
         args = [density, density, velocity, velocity, magnetic, magnetic, *polar, *sides, *mids]
         specs = [one(NPOL), one(NPOL, tiles - 1), three(NPOL), three(NPOL, tiles - 1),
                  three(NPOL), three(NPOL, tiles - 1)]
         for i, p in enumerate(polar):
             specs.append(pl.BlockSpec(
                 (4, 1, azimuth + HALO, NPOL),
-                lambda t, s, i=i: (0, jnp.clip(own(t, s) - s[2 + i], 0, chunk - 1), 0, 0)))
+                lambda t, s, i=i: (0, jnp.clip(own(t, s) - s[2 + i], 0, chunks[i] - 1), 0, 0)))
         specs += [side, side]
         mid_width = width - NPOL
         specs += [pl.BlockSpec((1, azimuth, mid_width), lambda t, s: (out(t, s), 0, 0)),
@@ -608,13 +630,13 @@
         if not middle:
             n = len(polar)
             ins = ins[:6] + (ins[6 : 6 + n],) + ins[6 + n :]
-        stencil_kernel(middle, radial, azimuth, chunk, starts, ins, spare, outs, scratch)
+        stencil_kernel(middle, radial, azimuth, chunks, starts, ins, spare, outs, scratch)
 
     rows = FRONT + azimuth + 2 * TILE
     scratch = (
         [pltpu.VMEM((8, rows, ring), jnp.float32)] * 7
         + [pltpu.VMEM((4, rows, ring), jnp.float32)] * 3
-        + [pltpu.VMEM((azimuth, ring), jnp.float32)] * 3
+        + [pltpu.VMEM((azimuth, ring), jnp.float32)] * 5
     )
     return pl.pallas_call(
         kernel,
@@ -652,20 +674,23 @@
     radial, azimuth, width = density.shape
     devices = lax.axis_size("phi")
     pairs = 4 * radial // devices
-    chunks = 2 if pairs % 2 == 0 else 1
-    layers = radial // chunks
+    shares = [pairs - 1, 1] if pairs > 1 else [pairs]
+    layers = [radial * n // pairs for n in shares]
+    split = len(shares) > 1
     low = lax.axis_index("row") == 0
     fields = (density, velocity, magnetic)
 
     def pick(a, b):
         return jnp.where(low, jnp.int32(a), jnp.int32(b))
 
-    def transpose(x, rows):
-        x = x.reshape(devices, pairs // chunks, rows, NPOL)
+    def transpose(x, share, rows):
+        x = x.reshape(devices, share, rows, NPOL)
         return lax.all_to_all(x, "phi", split_axis=0, concat_axis=0, tiled=True)
 
-    base = [pick(layers * (chunks - 1 - c), layers * c) for c in range(chunks)]
-    packed = [pack_lines(density, velocity, base[c], layers) for c in range(chunks)]
+    base = [pick(radial - layers[0], 0)]
+    if split:
+        base.append(pick(0, layers[0]))
+    packed = [pack_lines(density, velocity, b, n) for b, n in zip(base, layers)]
     first_rows, last_rows = pack_sides(density, velocity, magnetic)
 
     far, near, pair = pick(radial - 3, 0), pick(radial - 1, 0), pick(radial - 2, 0)
@@ -681,42 +706,42 @@
     around = [(i, (i + 1) % devices) for i in range(devices)]
     back = [(j, i) for i, j in around]
 
-    lines = [transpose(packed[0], azimuth)]
-    sides = (lax.ppermute(last_rows, "phi", around), lax.ppermute(first_rows, "phi", back))
-    if chunks > 1:
-        packed[1], sides, planes = lax.optimization_barrier((packed[1], sides, planes))
-        lines.append(transpose(packed[1], azimuth))
+    side_low = lax.ppermute(last_rows, "phi", around)
+    side_high = lax.ppermute(first_rows, "phi", back)
+    sides = (side_low, side_high)
+    lines = [transpose(packed[0], shares[0], azimuth)]
     planes = swap_rows(planes)
+
+    def starts(s):
+        return jnp.stack([s, s] + base)
+
+    deep = radial - REACH
+    mids = stencil(True, deep, starts(pick(0, REACH)), fields, sides)
+    if split:
+        packed[1], mids = lax.optimization_barrier((packed[1], tuple(mids)))
+        lines.append(transpose(packed[1], shares[1], azimuth))
     corner = swap_rows(
         jnp.concatenate([lax.dynamic_slice_in_dim(x, pair, 2, 0) for x in sides], axis=0))
 
-    def starts(s):
-        return jnp.stack([s, s] + base)
-
-    deep = radial - REACH
-    early = (deep + 1) // 2
-    mids = stencil(True, early, starts(pick(0, REACH)), fields, sides)
     smooth = [filter_lines(x, width) for x in lines]
-    smooth[0], mids = lax.optimization_barrier((smooth[0], tuple(mids)))
-    polar = [transpose(smooth[0], azimuth + HALO)]
-    mids = stencil(True, deep - early, starts(pick(early, early + REACH)), fields, sides, into=mids)
-    if chunks > 1:
+    polar = [transpose(smooth[0], shares[0], azimuth + HALO)]
+    mids = stencil(True, REACH, starts(pick(deep, 0)), fields, sides,
+                   ghosts=(planes, corner, None), into=mids)
+    if split:
         smooth[1], mids = lax.optimization_barrier((smooth[1], tuple(mids)))
-        polar.append(transpose(smooth[1], azimuth + HALO))
-    polar = [p.reshape(4, layers, azimuth + HALO, NPOL) for p in polar]
+        polar.append(transpose(smooth[1], shares[1], azimuth + HALO))
+    polar = [p.reshape(4, n, azimuth + HALO, NPOL) for p, n in zip(polar, layers)]
 
     first = polar[0]
-    far, near = pick(layers - 3, 0), pick(layers - 1, 0)
+    far, near = pick(layers[0] - 3, 0), pick(layers[0] - 1, 0)
     sent = lax.dynamic_slice_in_dim(first[:2], far, 3, 1).reshape(6, azimuth + HALO, NPOL)
     close = lax.dynamic_slice_in_dim(first[2:], near, 1, 1).reshape(2, azimuth + HALO, NPOL)
     filtered = swap_rows(jnp.concatenate([sent, close], axis=0))
-    mids = stencil(True, REACH, starts(pick(deep, 0)), fields, sides,
-                   ghosts=(planes, corner, None), into=mids)
-
-    edge = radial // 2 - REACH
+
+    edge = layers[0] - REACH
     out = stencil(False, edge, starts(pick(radial - edge, 0)), fields, sides,
                   ghosts=(planes, corner, filtered), polar=polar[:1], mids=mids)
-    if chunks > 1:
+    if split:
         polar[1], out = lax.optimization_barrier((polar[1], tuple(out)))
     out = stencil(False, radial - edge, starts(pick(0, edge)), fields, sides, polar=polar,
                   mids=mids, into=out)

time: 362 us -> 358 us (0.989)
  Pallas kernels: 194 us -> 158 us
  waiting for transfers between devices: 103 us -> 134 us
    pallas_call x5 -> x4, Pallas kernels: 164 us -> 125 us  [stencil(): pl.pallas_call(kernel, grid_spec=pltpu.PrefetchScalarGridSpec(num_scalar_...]
    ppermute x2, waiting for transfers between devices: 22.9 us -> 50.6 us  [the longest x1 50.6 us: section(): side_low = lax.ppermute(last_rows, 'phi', around)]
    all_to_all x4, waiting for transfers between devices: 2.72 us -> 9.29 us  [transpose(): return lax.all_to_all(x, 'phi', split_axis=0, concat_axis=0, tiled=True)]
    unnamed x12 -> x16, local copies, waits for them, and re-layouts: 9.33 us -> 9.57 us
  transfers between devices with their start and end apart: 9 -> 9, of which waited for: 4 -> 4; matrix products, arithmetic and copies ran while one was open for 4% -> 3% of each run, Pallas kernels for 40% -> 36%
where the time goes in v1:
time: 358 us; the launch traced here: 357 us
  Pallas kernels  158 us (44%)
  waiting for transfers between devices  134 us (37%)
  starting transfers between devices  46.4 us (13%)
  local copies, waits for them, and re-layouts  14.6 us (4%)
    pallas_call x4, Pallas kernels, stencil(): pl.pallas_call(kernel, grid_spec=pltpu.PrefetchScalarGridSpec(num_scalar_...  125 us
    ppermute x3, waiting for transfers between devices, swap_rows(): return lax.ppermute(x, 'row', [(0, 1), (1, 0)])  74 us
    ppermute x1, waiting for transfers between devices, section(): side_low = lax.ppermute(last_rows, 'phi', around)  50.6 us
    all_to_all x4, starting transfers between devices, transpose(): return lax.all_to_all(x, 'phi', split_axis=0, concat_axis=0, tiled=True)  37.5 us
    pallas_call x2, Pallas kernels, filter_lines(): pl.pallas_call(lambda *refs: filter_kernel(group, inner, blocks, *refs),...  20.9 us
    unnamed x16, local copies, waits for them, and re-layouts  9.57 us
    all_to_all x4, waiting for transfers between devices, transpose(): return lax.all_to_all(x, 'phi', split_axis=0, concat_axis=0, tiled=True)  9.29 us
    pallas_call x2, Pallas kernels, pack_lines(): pl.pallas_call(kernel, grid_spec=pltpu.PrefetchScalarGridSpec(num_scalar_...  7.95 us
  transfers between devices with their start and end apart: 9, of which 4 were waited for; matrix products, arithmetic and copies ran while one was open for 3% of the time, Pallas kernels for 36%

profile of v1, /device:TPU:0, one launch (start us, length us, event | category | flops | bytes accessed | tf_op | source)
XLA Modules:
  0.0 356.6 jit_solution(1488151933176272478)
XLA Ops:
  0.6 5.3 %pack_lines.2 = f32[4,12,128,128]{3,2,1,0:T(8,128)} custom-call(s32[1]{0:T(128)} %bitcast.3.start, f32[16,128,512]{2,1,0:T(8,128)} %refs_1_.9, f32[16,128,512]{2,1,0:T(8,128)} %refs_1_.9, f32[3,16,128,512]{3,2,1,0:T(8,128)} %refs_3_.3, f32[3,16,128,512]{3,2,1,0:T(8,128)} %refs_3_.3), custom_call_target="tpu_custom_call" | custom-call | tf_op jit(solution)/shard_map/pack_lines/pallas_call | solution.py:208
  5.9 7.4 %all-to-all-start = ((f32[16,3,128,128]{3,2,1,0:T(8,128)}), f32[16,3,128,128]{3,2,1,0:T(8,128)}, u32[]{:S(2)}, u32[]{:S(2)}) async-start(f32[16,3,128,128]{3,2,1,0:T(8,128)} %bitcast.27), calls=%async_computation | async-start | bytes 6291456 | tf_op jit(solution)/shard_map/all_to_all | solution.py:688
  13.4 4.0 %pack_sides.1 = (f32[16,16,512]{2,1,0:T(8,128)}, f32[16,16,512]{2,1,0:T(8,128)}) custom-call(f32[16,128,512]{2,1,0:T(8,128)} %refs_1_.9, f32[16,128,512]{2,1,0:T(8,128)} %refs_1_.9, f32[3,16,128,512]{3,2,1,0:T(8,128)} %refs_3_.3, f32[3,16,128,512]{3,2,1,0:T(8,128)} %refs_3_.3, f32[3,16,128,512]{3,2,1,0:T(8,128)} %refs_5_.3, f32[3,16,128,512]{3,2,1,0:T(8,128)} %refs_5_.3), custom_call_target="tpu_custom_call" | custom-call | tf_op jit(solution)/shard_map/pack_sides/pallas_call | solution.py:244
  17.4 0.3 collective-permute-start
  17.8 4.1 %collective-permute-start.1 = (f32[16,16,512]{2,1,0:T(8,128)}, f32[16,16,512]{2,1,0:T(8,128)S(1)}, u32[]{:S(2)}, u32[]{:S(2)}) collective-permute-start(f32[16,16,512]{2,1,0:T(8,128)} %get-tuple-element.20), channel_id=1, source_target_pairs={{1,0},{2,1},{3,2},{4,3},{5,4},{6,5},{7,6},{8,7},{9,8},{10,9},{11,1... | collective-permute-start | bytes 1572872 | tf_op jit(solution)/shard_map/ppermute | solution.py:710
  21.9 2.7 pack_lines.3
  24.5 0.6 add_add_fusion.1.starts
  25.1 50.6 %collective-permute-done.refs_3_.refs_7_.refs_8_ = f32[16,16,512]{2,1,0:T(8,128)S(1)} collective-permute-done((f32[16,16,512]{2,1,0:T(8,128)}, f32[16,16,512]{2,1,0:T(8,128)S(1)}, u32[]{:S(2)}, u32[]{:S(2)}) %collective-permute-start) | collective-permute-done | bytes 524320 | tf_op jit(solution)/shard_map/ppermute | solution.py:709
  75.7 0.0 copy-start
  75.7 0.0 collective-permute-done.1.refs_4_.refs_8_.refs_9_
  75.7 0.8 copy-done
  76.5 0.0 copy-start.1
  76.5 0.8 copy-done.1
  77.3 49.5 %section_mid.2 = (f32[16,128,384]{2,1,0:T(8,128)}, f32[3,16,128,384]{3,2,1,0:T(8,128)}) custom-call(s32[4]{0:T(128)} %add_add_fusion.1.starts, f32[16,128,512]{2,1,0:T(8,128)} %refs_1_.9, f32[3,16,128,512]{3,2,1,0:T(8,128)} %refs_3_.3, f32[3,16,128,512]{3,2,1,0:T(8,128)} %refs_5_.3, f32[16,16,512]{2,1,0:T(8,128)} %copy-done, f32[16,16,512]{2,1,0:T(8,128)} %copy-done.1), custom_call_target="tpu_custom_call" | custom-call | flops 638976000 | bytes 40894464 | tf_op jit(solution)/shard_map/section_mid/pallas_call | solution.py:641
  126.8 0.0 all-to-all-done.refs_0_
  126.8 17.6 %all-to-all-start.2 = ((f32[16,1,128,128]{3,2,1,0:T(8,128)}), f32[16,1,128,128]{3,2,1,0:T(8,128)S(1)}, u32[]{:S(2)}, u32[]{:S(2)}) async-start(f32[16,1,128,128]{3,2,1,0:T(8,128)} %bitcast.29), calls=%async_computation.2 | async-start | bytes 2097152 | tf_op jit(solution)/shard_map/all_to_all | solution.py:688
  144.4 13.6 %polar_filter.2 = f32[16,3,136,128]{3,2,1,0:T(8,128)} custom-call(f32[16,3,128,128]{3,2,1,0:T(8,128)} %all-to-all-done.refs_0_, f32[9,256,256]{2,1,0:T(8,128)} %constant.61.clone.refs_1_, f32[9,128,128]{2,1,0:T(8,128)} %constant.62.clone.refs_2_), custom_call_target="tpu_custom_call" | custom-call | flops 3221225472 | bytes 6291456 | tf_op jit(solution)/shard_map/polar_filter/pallas_call | solution.py:171
  158.0 9.3 %all-to-all-done.2.refs_0_ = f32[16,1,128,128]{3,2,1,0:T(8,128)S(1)} async-done(((f32[16,1,128,128]{3,2,1,0:T(8,128)}), f32[16,1,128,128]{3,2,1,0:T(8,128)S(1)}, u32[]{:S(2)}, u32[]{:S(2)}) %all-to-all-start.2) | async-done | bytes 1048608 | tf_op jit(solution)/shard_map/all_to_all | solution.py:688
  167.3 1.0 copy-done.4
  168.2 6.8 %all-to-all-start.1 = ((f32[16,3,136,128]{3,2,1,0:T(8,128)}), f32[16,3,136,128]{3,2,1,0:T(8,128)}, u32[]{:S(2)}, u32[]{:S(2)}) async-start(f32[16,3,136,128]{3,2,1,0:T(8,128)} %polar_filter.2), calls=%async_computation.1 | async-start | bytes 6684672 | tf_op jit(solution)/shard_map/all_to_all | solution.py:688
  175.1 1.2 dynamic-slice_dynamic-update-slice_fusion
  176.3 1.2 bitcast_dynamic-update-slice_fusion
  177.5 1.1 bitcast_dynamic-update-slice_fusion.3
  178.6 1.1 bitcast_dynamic-update-slice_fusion.2
  179.6 1.1 bitcast_dynamic-update-slice_fusion.1
  180.7 2.8 collective-permute-start.2
  183.5 0.8 constant_dynamic-slice_fusion.2
  184.4 0.8 constant_dynamic-slice_fusion.1
  185.2 0.1 collective-permute-start.3
  185.3 0.6 add_add_fusion.2.starts
  185.9 7.3 %polar_filter.3 = f32[16,1,136,128]{3,2,1,0:T(8,128)} custom-call(f32[16,1,128,128]{3,2,1,0:T(8,128)} %copy-done.4, f32[9,256,256]{2,1,0:T(8,128)} %constant.61.clone.refs_1_, f32[9,128,128]{2,1,0:T(8,128)} %constant.62.clone.refs_2_), custom_call_target="tpu_custom_call" | custom-call | flops 1073741824 | bytes 2097152 | tf_op jit(solution)/shard_map/polar_filter/pallas_call | solution.py:171
  193.2 61.8 %collective-permute-done.3.refs_12_.refs_13_.refs_18_.refs_19_ = f32[4,16,512]{2,1,0:T(8,128)S(1)} collective-permute-done((f32[4,16,512]{2,1,0:T(8,128)S(1)}, f32[4,16,512]{2,1,0:T(8,128)S(1)}, u32[]{:S(2)}, u32[]{:S(2)}) %collective-permute-start.3) | collective-permute-done | bytes 131104 | tf_op jit(solution)/shard_map/ppermute | solution.py:670
  255.0 0.0 collective-permute-done.2.refs_5_.refs_6_.refs_7_.refs_8_.refs_9_.refs_10_.refs_11_.refs_12_.refs_13_.refs_14_.refs_15_.refs_16_.refs_17_
  255.0 0.6 copy-done.5
  255.6 19.6 %section_mid.3 = (f32[16,128,384]{2,1,0:T(8,128)}, f32[3,16,128,384]{3,2,1,0:T(8,128)}) custom-call(s32[4]{0:T(128)} %add_add_fusion.2.starts, f32[16,128,512]{2,1,0:T(8,128)} %refs_1_.9, f32[3,16,128,512]{3,2,1,0:T(8,128)} %refs_3_.3, f32[3,16,128,512]{3,2,1,0:T(8,128)} %refs_5_.3, ...), custom_call_target="tpu_custom_call", output_to_operand_aliasing={{0}: (15, {}), {1}: (16, {})} | custom-call | flops 147456000 | bytes 9437184 | tf_op jit(solution)/shard_map/section_mid/pallas_call | solution.py:641
  275.2 0.0 all-to-all-done.1
  275.2 5.7 %all-to-all-start.3 = ((f32[16,1,136,128]{3,2,1,0:T(8,128)}), f32[16,1,136,128]{3,2,1,0:T(8,128)S(1)}, u32[]{:S(2)}, u32[]{:S(2)}) async-start(f32[16,1,136,128]{3,2,1,0:T(8,128)} %polar_filter.3), calls=%async_computation.3 | async-start | bytes 2228224 | tf_op jit(solution)/shard_map/all_to_all | solution.py:688
  280.9 2.2 fusion
  283.2 1.5 collective-permute-start.4
  284.7 0.6 add_add_fusion.starts
  285.4 0.6 add_add_fusion.3.starts
  286.0 12.3 %collective-permute-done.4.refs_20_.refs_21_.refs_22_.refs_23_ = f32[8,136,128]{2,1,0:T(8,128)S(1)} collective-permute-done((f32[8,136,128]{2,1,0:T(8,128)S(1)}, f32[8,136,128]{2,1,0:T(8,128)S(1)}, u32[]{:S(2)}, u32[]{:S(2)}) %collective-permute-start.4) | collective-permute-done | bytes 557088 | tf_op jit(solution)/shard_map/ppermute | solution.py:670
  298.2 0.8 copy-done.2
  299.0 31.9 %section_polar.2 = (f32[16,128,512]{2,1,0:T(8,128)}, f32[3,16,128,512]{3,2,1,0:T(8,128)}) custom-call(s32[4]{0:T(128)} %add_add_fusion.3.starts, f32[16,128,512]{2,1,0:T(8,128)} %refs_1_.9, f32[16,128,512]{2,1,0:T(8,128)} %refs_1_.9, f32[3,16,128,512]{3,2,1,0:T(8,128)} %refs_3_.3, f32[3,16,128,512]{3,2,1,0:T(8,128)} %refs_3_.3, f32[3,16,128,512]{3,2,1,0:T(8,128)} %refs_5_.3, ...), custom_call_target="tpu_custom_call" | custom-call | flops 294912000 | bytes 28311552 | tf_op jit(solution)/shard_map/section_polar/pallas_call | solution.py:641
  330.9 0.0 all-to-all-done.3
  331.0 0.0 copy-start.3
  331.0 1.0 copy-done.3
  332.0 24.5 %section_polar.3 = (f32[16,128,512]{2,1,0:T(8,128)}, f32[3,16,128,512]{3,2,1,0:T(8,128)}) custom-call(s32[4]{0:T(128)} %add_add_fusion.starts, f32[16,128,512]{2,1,0:T(8,128)} %refs_1_.9, f32[16,128,512]{2,1,0:T(8,128)} %refs_1_.9, f32[3,16,128,512]{3,2,1,0:T(8,128)} %refs_3_.3, ...), custom_call_target="tpu_custom_call", output_to_operand_aliasing={{0}: (13, {}), {1}: (14, {})} | custom-call | flops 229376000 | bytes 22020096 | tf_op jit(solution)/shard_map/section_polar/pallas_call | solution.py:641
  (7 shorter events, 0.1 us)
Async XLA Ops:
  5.9 120.9 %all-to-all-start = ((f32[16,3,128,128]{3,2,1,0:T(8,128)}), f32[16,3,128,128]{3,2,1,0:T(8,128)}, u32[]{:S(2)}, u32[]{:S(2)}) async-start(f32[16,3,128,128]{3,2,1,0:T(8,128)} %bitcast.27), calls=%async_computation | async-start | bytes 6291456 | tf_op jit(solution)/shard_map/all_to_all | solution.py:688
  17.4 58.3 %collective-permute-start = (f32[16,16,512]{2,1,0:T(8,128)}, f32[16,16,512]{2,1,0:T(8,128)S(1)}, u32[]{:S(2)}, u32[]{:S(2)}) collective-permute-start(f32[16,16,512]{2,1,0:T(8,128)} %get-tuple-element.19), channel_id=1, source_target_pairs={{0,1},{1,2},{2,3},{3,4},{4,5},{5,6},{6,7},{7,8},{8,9},{9,10},{10,1... | collective-permute-start | bytes 1572872 | tf_op jit(solution)/shard_map/ppermute | solution.py:709
  17.8 57.9 %collective-permute-start.1 = (f32[16,16,512]{2,1,0:T(8,128)}, f32[16,16,512]{2,1,0:T(8,128)S(1)}, u32[]{:S(2)}, u32[]{:S(2)}) collective-permute-start(f32[16,16,512]{2,1,0:T(8,128)} %get-tuple-element.20), channel_id=1, source_target_pairs={{1,0},{2,1},{3,2},{4,3},{5,4},{6,5},{7,6},{8,7},{9,8},{10,9},{11,1... | collective-permute-start | bytes 1572872 | tf_op jit(solution)/shard_map/ppermute | solution.py:710
  75.7 0.8 copy-start
  76.5 0.8 copy-start.1
  126.8 40.5 %all-to-all-start.2 = ((f32[16,1,128,128]{3,2,1,0:T(8,128)}), f32[16,1,128,128]{3,2,1,0:T(8,128)S(1)}, u32[]{:S(2)}, u32[]{:S(2)}) async-start(f32[16,1,128,128]{3,2,1,0:T(8,128)} %bitcast.29), calls=%async_computation.2 | async-start | bytes 2097152 | tf_op jit(solution)/shard_map/all_to_all | solution.py:688
  167.3 1.0 copy-start.4
  168.2 107.0 %all-to-all-start.1 = ((f32[16,3,136,128]{3,2,1,0:T(8,128)}), f32[16,3,136,128]{3,2,1,0:T(8,128)}, u32[]{:S(2)}, u32[]{:S(2)}) async-start(f32[16,3,136,128]{3,2,1,0:T(8,128)} %polar_filter.2), calls=%async_computation.1 | async-start | bytes 6684672 | tf_op jit(solution)/shard_map/all_to_all | solution.py:688
  180.7 74.2 %collective-permute-start.2 = (f32[12,128,512]{2,1,0:T(8,128)S(1)}, f32[12,128,512]{2,1,0:T(8,128)}, u32[]{:S(2)}, u32[]{:S(2)}) collective-permute-start(f32[12,128,512]{2,1,0:T(8,128)S(1)} %bitcast_dynamic-update-slice_fusion.1), channel_id=1, source_target_pairs={{0,16},{16,0},{1,17},{17,1},{2,18},{18,2},{3,19},{19,3},{4,20},{20... | collective-permute-start | bytes 9437192 | tf_op jit(solution)/shard_map/ppermute | solution.py:670
  185.2 69.7 %collective-permute-start.3 = (f32[4,16,512]{2,1,0:T(8,128)S(1)}, f32[4,16,512]{2,1,0:T(8,128)S(1)}, u32[]{:S(2)}, u32[]{:S(2)}) collective-permute-start(f32[4,16,512]{2,1,0:T(8,128)S(1)} %pad_maximum_fusion.1), channel_id=1, source_target_pairs={{0,16},{16,0},{1,17},{17,1},{2,18},{18,2},{3,19},{19,3},{4,20},{20... | collective-permute-start | bytes 393224 | tf_op jit(solution)/shard_map/ppermute | solution.py:670
  255.0 0.7 copy-start.5
  275.2 55.7 %all-to-all-start.3 = ((f32[16,1,136,128]{3,2,1,0:T(8,128)}), f32[16,1,136,128]{3,2,1,0:T(8,128)S(1)}, u32[]{:S(2)}, u32[]{:S(2)}) async-start(f32[16,1,136,128]{3,2,1,0:T(8,128)} %polar_filter.3), calls=%async_computation.3 | async-start | bytes 2228224 | tf_op jit(solution)/shard_map/all_to_all | solution.py:688
  283.2 15.0 %collective-permute-start.4 = (f32[8,136,128]{2,1,0:T(8,128)S(1)}, f32[8,136,128]{2,1,0:T(8,128)S(1)}, u32[]{:S(2)}, u32[]{:S(2)}) collective-permute-start(f32[8,136,128]{2,1,0:T(8,128)S(1)} %pad_maximum_fusion), channel_id=1, source_target_pairs={{0,16},{16,0},{1,17},{17,1},{2,18},{18,2},{3,19},{19,3},{4,20},{20... | collective-permute-start | bytes 1671176 | tf_op jit(solution)/shard_map/ppermute | solution.py:670
  298.2 0.8 copy-start.2
  331.0 1.0 copy-start.3
